TPU v7x, 256 devices: a whole 4x4x8 slice. The times are simulated.
256 devices in a mesh: gx: 16 (over x, z_lo, core), gy: 16 (over y, z_hi).
Axes of the slice: x: 4, y: 4, z: 8 (z_hi: 4, z_lo: 2; z = z_hi * 2 + z_lo), core: 2. Of those that a mesh axis runs over, the one named last changes fastest.
Arguments:
- tokens: bfloat16 [131072, 1280], P(('gx', 'gy')), may hold values from -6 to 6
- out_grad: bfloat16 [131072, 1280], P(('gx', 'gy')), may hold values from -400 to 400
- segments: int32 [256, 512], P(('gx', 'gy')), may hold values from 0 to 7, never falling along the last dimension, each value on 1 to 256 neighbouring positions
- pos_rows: int32 [131072], P(('gx', 'gy')), may hold values from 0 to 15
- pos_cols: int32 [131072], P(('gx', 'gy')), may hold values from 0 to 15
- row_table: bfloat16 [16, 1280], replicated, may hold values from -4 to 4
- col_table: bfloat16 [16, 1280], replicated, may hold values from -4 to 4
- norm_gain: float32 [1280], replicated, may hold values from 0.25 to 1.75
- master_up: float32 [1280, 2560], P('gx'), may hold values from -0.15625 to 0.15625
- master_down: float32 [1280, 2560], P('gx'), may hold values from -0.125 to 0.125
- moment_up: float32 [1280, 2560], P('gx'), may hold values from -6 to 6
- moment_down: float32 [1280, 2560], P('gx'), may hold values from -6 to 6
Outputs:
- new_master_up: float32 [1280, 2560], P('gx')
- new_master_down: float32 [1280, 2560], P('gx')
- new_moment_up: float32 [1280, 2560], P('gx')
- new_moment_down: float32 [1280, 2560], P('gx')
Inputs may be any that keep to these rules, and one draw needn't show every extreme that they name: `segments`: each replica's 512 tokens hold all 8 images in order, each of 1 to 256 tokens.
All inputs are finite; a program needn't handle non-finite values.
Results may differ from a plain program's by a relative error of at most 0.02.
Values may be sent and summed in bfloat16 or wider, within the bound.
No kernel may reach another device: no remote copies, remote signals or barrier semaphores. Data moves between devices by JAX's collectives and lax.ppermute only.
A program may use at most 128 MiB of HBM per device.

v0:
```python
import jax
import jax.numpy as jnp
from jax import lax
from jax.sharding import Mesh
from jax.sharding import PartitionSpec as P

D = 1280
FF = 2560
GRID = 16
IMGS = 8
GX = ("gx_0", "gx_1", "gx_2")
GY = ("gy_0", "gy_1")
GX_GY = ("gx_0", "gx_1", "gx_2", "gy_0", "gy_1")
momentum_keep = 0.9
learn_rate = 0.01


def in_blocks(value, dim, size):
    lengths = value.shape
    pieces = value.reshape(*lengths[:dim], size, lengths[dim] // size, *lengths[dim + 1 :])
    return jnp.moveaxis(pieces, dim, 0)


def sent_and_summed(value, axis, dim):
    size = lax.axis_size(axis)
    pieces = lax.all_to_all(in_blocks(value, dim, size), axis, 0, 0, tiled=True)
    return jnp.sum(pieces.astype(jnp.float32), axis=0)


def over_axes(value, axes):
    for axis in axes:
        value = lax.psum(value, axis)
    return value


def gather_turned(arrays, axis, dims):
    turned = [jnp.moveaxis(a, dim, 0) for a, dim in zip(arrays, dims)]
    widths = [t[0].size for t in turned]
    both = jnp.concatenate([t.reshape(-1, w) for t, w in zip(turned, widths)], axis=1)
    out = lax.all_gather(both, axis, axis=0, tiled=True)
    pieces = jnp.split(out, [sum(widths[:k]) for k in range(1, len(widths))], axis=1)
    return tuple(
        (
            jnp.moveaxis(b.reshape(-1, *t.shape[1:]), 0, dim)
            for b, t, dim in zip(pieces, turned, dims)
        )
    )


def gelu_tanh(values):
    return (
        0.5
        * values
        * (1.0 + jnp.tanh(0.7978845608 * (values + 0.044715 * values * values * values)))
    )


def table_lookup(positions, table):
    onehot = (positions[:, None] == jnp.arange(GRID, dtype=jnp.int32)[None, :]).astype(jnp.bfloat16)
    return jnp.dot(onehot, table, preferred_element_type=jnp.float32)


def column_product(left, right):
    return lax.dot_general(
        left, right, (((0,), (0,)), ((), ())), preferred_element_type=jnp.float32
    )


def on_device(
    tokens,
    out_grad,
    segments,
    pos_rows,
    pos_cols,
    row_table,
    col_table,
    norm_gain,
    master_up,
    master_down,
    moment_up,
    moment_down,
):
    embedded = (
        tokens.astype(jnp.float32)
        + table_lookup(pos_rows, row_table)
        + table_lookup(pos_cols, col_table)
    )
    average = jnp.mean(embedded, axis=1, keepdims=True)
    centered = embedded - average
    variance = jnp.mean(centered * centered, axis=1, keepdims=True)
    normed = (centered * lax.rsqrt(variance + 1e-06) * norm_gain[None, :]).astype(jnp.bfloat16)
    member = (segments[0][:, None] == jnp.arange(IMGS, dtype=jnp.int32)[None, :]).astype(
        jnp.float32
    )
    per_image = 1.0 / jnp.sum(member, axis=0)
    token_weight = jnp.dot(member, per_image)
    weighted = (out_grad.astype(jnp.float32) * token_weight[:, None]).astype(jnp.bfloat16)
    left_cols = normed
    pre_act = jnp.dot(
        left_cols,
        lax.all_gather(master_up.astype(jnp.bfloat16), GX, axis=0, tiled=True),
        preferred_element_type=jnp.float32,
    )
    hidden = gelu_tanh(pre_act).astype(jnp.bfloat16)
    left_cols = weighted
    hidden_grad = jnp.dot(
        left_cols,
        lax.all_gather(master_down.astype(jnp.bfloat16), GX, axis=0, tiled=True),
        preferred_element_type=jnp.float32,
    )
    _, backward = jax.vjp(gelu_tanh, pre_act)
    pre_grad = backward(hidden_grad)[0].astype(jnp.bfloat16)
    group_sum = lax.psum_scatter(
        jnp.concatenate(
            [column_product(normed, pre_grad), column_product(weighted, hidden)], axis=1
        ).astype(jnp.bfloat16),
        GX,
        scatter_dimension=0,
        tiled=True,
    )
    moments = jnp.concatenate([moment_up, moment_down], axis=1)
    masters = jnp.concatenate([master_up, master_down], axis=1)
    entries = 2.0 * D * FF
    grad_share = sent_and_summed(group_sum, GY, 1)
    share_width = grad_share.shape[1]
    offset = lax.axis_index(GY) * share_width
    moment_share = lax.dynamic_slice_in_dim(moments, offset, share_width, 1)
    master_share = lax.dynamic_slice_in_dim(masters, offset, share_width, 1)
    squares = over_axes(jnp.sum(grad_share * grad_share), GX_GY)
    scale = lax.rsqrt(squares / entries + 1e-06)
    new_moment_share = momentum_keep * moment_share + scale * grad_share
    new_master_share = master_share - learn_rate * new_moment_share
    new_masters, new_moments = tuple(
        (
            part.astype(jnp.float32)
            for part in gather_turned(
                (new_master_share.astype(jnp.bfloat16), new_moment_share.astype(jnp.bfloat16)),
                GY,
                (1, 1),
            )
        )
    )
    half = master_up.shape[1]
    return (
        new_masters[:, :half],
        new_masters[:, half:],
        new_moments[:, :half],
        new_moments[:, half:],
    )


def solution(mesh):
    split = Mesh(mesh.devices.reshape(4, 2, 2, 4, 4), ("gx_0", "gx_1", "gx_2", "gy_0", "gy_1"))
    return jax.shard_map(
        on_device,
        mesh=split,
        in_specs=(
            P(GX_GY, None),
            P(GX_GY, None),
            P(GX_GY, None),
            P(GX_GY),
            P(GX_GY),
            P(),
            P(),
            P(),
            P(GX, None),
            P(GX, None),
            P(GX, None),
            P(GX, None),
        ),
        out_specs=(P(GX, None), P(GX, None), P(GX, None), P(GX, None)),
        check_vma=False,
    )
```

profile of v0, /device:TPU:2, one launch (start us, length us, event | category | flops | bytes accessed | tf_op | source)
XLA Modules:
  0.0 433.7 jit_solution(8038855572694189824)
XLA Ops:
  7.2 0.0 copy-start
  7.2 0.0 all-gather.5.cloned.1.call-start
  7.2 1.9 convert_element_type.53
  9.2 0.0 all-gather.5.cloned.1.call-update
  9.2 0.0 all-gather.7.cloned.1.call-start
  9.3 1.9 convert_element_type.57
  11.2 0.0 all-gather.7.cloned.1.call-update
  11.2 0.0 reduce-scatter.2.cloned.1.call-start
  11.3 0.8 convert_reduce_fusion.1
  12.1 0.0 copy-start.7
  12.1 1.9 convolution_add_fusion.1
  14.0 0.7 fusion.37
  14.7 0.4 multiply_reduce_fusion
  15.1 0.1 fusion.21
  15.3 44.0 %all-gather.5.cloned.1.call-done = bf16[1280,2560]{1,0:T(8,128)(2,1)} async-done(((bf16[80,2560]{1,0:T(8,128)(2,1)}), bf16[1280,2560]{1,0:T(8,128)(2,1)}) %all-gather.5.cloned.1.call-update) | async-done | bytes 6553616 | tf_op jit(solution)/shard_map/all_gather | solution.py:101
  59.3 0.0 copy-done.7
  59.3 6.0 %fusion.33 = f32[512,2560]{1,0:T(8,128)S(1)} fusion(bf16[1280,2560]{1,0:T(8,128)(2,1)} %all-gather.5.cloned.1.call-done, f32[512,1280]{1,0:T(8,128)S(1)} %get-tuple-element.13, f32[1280]{0:T(1024)S(1)} %copy-done.7, f32[512]{0:T(512)S(1)} %add_rsqrt_fusion, f32[512]{0:T(512)S(1)} %broadcast_multiply_fusion), kind=kOutput, calls=%fused_computation.63 | convolution fusion | flops 3358064640 | bytes 14427136 | tf_op jit(solution)/shard_map/dot_general | solution.py:99
  65.3 2.4 copy-done.8
  67.7 0.0 copy-done.6
  67.7 6.0 %convolution_convert_fusion = bf16[1280,2560]{1,0:T(8,128)(2,1)} fusion(f32[512,2560]{1,0:T(8,128)S(1)} %fusion.33, bf16[512,1280]{1,0:T(8,128)(2,1)S(1)} %copy-done.6, f32[512]{0:T(512)S(1)} %bitcast.28), kind=kOutput, calls=%fused_computation.1 | convolution fusion | flops 3372482560 | bytes 13109248 | tf_op jit(solution)/shard_map/dot_general | solution.py:64
  73.7 34.9 %all-gather.7.cloned.1.call-done = bf16[1280,2560]{1,0:T(8,128)(2,1)} async-done(((bf16[80,2560]{1,0:T(8,128)(2,1)}), bf16[1280,2560]{1,0:T(8,128)(2,1)}) %all-gather.7.cloned.1.call-update) | async-done | bytes 6553616 | tf_op jit(solution)/shard_map/all_gather | solution.py:108
  108.6 14.3 %convolution_convert_fusion.1 = bf16[1280,2560]{1,0:T(8,128)(2,1)} fusion(f32[512,2560]{1,0:T(8,128)} %copy-done.8, bf16[1280,2560]{1,0:T(8,128)(2,1)} %all-gather.7.cloned.1.call-done, bf16[512,1280]{1,0:T(8,128)(2,1)} %param.13, f32[512]{0:T(512)S(1)} %bitcast.29, f32[512,1280]{1,0:T(8,128)S(1)} %get-tuple-element.13, f32[1280]{0:T(1024)S(1)} %copy-done.7, ...), kind=kOutput, calls=%fused_computation.2 | convolution fusion | flops 6750208000 | bytes 22293504 | tf_op jit(solution)/shard_map/dot_general | solution.py:64
  122.9 12.2 %pad_maximum_fusion = bf16[1280,5120]{1,0:T(8,128)(2,1)} fusion(bf16[1280,2560]{1,0:T(8,128)(2,1)} %convolution_convert_fusion, bf16[1280,2560]{1,0:T(8,128)(2,1)} %convolution_convert_fusion.1), kind=kLoop, calls=%fused_computation | loop fusion | flops 26214400 | bytes 26214400 | tf_op jit(solution)/shard_map/concatenate | solution.py:114
  135.2 0.0 reduce-scatter.2.cloned.1.call-update
  135.2 0.0 copy-start.2
  135.2 0.0 copy-start.3
  135.2 146.8 %reduce-scatter.2.cloned.1.call-done = bf16[80,5120]{1,0:T(8,128)(2,1)} async-done(((bf16[1280,5120]{1,0:T(8,128)(2,1)}), bf16[80,5120]{1,0:T(8,128)(2,1)}) %reduce-scatter.2.cloned.1.call-update) | async-done | bytes 819216 | tf_op jit(solution)/shard_map/reduce_scatter | solution.py:113
  282.1 1.9 reshape.28
  284.0 1.2 copy.23
  285.1 8.7 %all-to-all-start = ((bf16[16,80,320]{2,1,0:T(8,128)(2,1)}), bf16[16,80,320]{2,1,0:T(8,128)(2,1)S(1)}, u32[]{:S(2)}, u32[]{:S(2)}) async-start(bf16[16,80,320]{2,1,0:T(8,128)(2,1)} %bitcast.24), calls=%async_computation.1 | async-start | bytes 1966080 | tf_op jit(solution)/shard_map/all_to_all | solution.py:26
  293.8 0.2 all-gather.9.cloned.1.call-start
  294.1 23.3 %all-to-all-done = bf16[16,80,320]{2,1,0:T(8,128)(2,1)S(1)} async-done(((bf16[16,80,320]{2,1,0:T(8,128)(2,1)}), bf16[16,80,320]{2,1,0:T(8,128)(2,1)S(1)}, u32[]{:S(2)}, u32[]{:S(2)}) %all-to-all-start) | async-done | bytes 819232 | tf_op jit(solution)/shard_map/all_to_all | solution.py:26
  317.4 0.2 convert_reduce_fusion
  317.5 0.6 multiply_reduce_fusion.1
  318.2 15.4 %psum.35 = f32[]{:T(128)} all-reduce(f32[]{:T(128)} %multiply_reduce_fusion.1), channel_id=1, replica_groups=mesh['gx_0'=4,'gx_1'=2,'gx_2'=2,'gy_0'=4,'gy_1'=4] {'gx_0'}, use_global_device_ids=true, to_apply=%region_6.0 | all-reduce | flops 1 | bytes 8 | tf_op jit(solution)/shard_map/psum | solution.py:32
  333.6 5.5 %psum.36 = f32[]{:T(128)} all-reduce(f32[]{:T(128)} %psum.35), channel_id=1, replica_groups=mesh['gx_0'=4,'gx_1'=2,'gx_2'=2,'gy_0'=4,'gy_1'=4] {'gx_1'}, use_global_device_ids=true, to_apply=%region_7.0 | all-reduce | flops 1 | bytes 8 | tf_op jit(solution)/shard_map/psum | solution.py:32
  339.1 3.1 psum.37
  342.2 8.9 %psum.38 = f32[]{:T(128)} all-reduce(f32[]{:T(128)} %psum.37), channel_id=1, replica_groups=mesh['gx_0'=4,'gx_1'=2,'gx_2'=2,'gy_0'=4,'gy_1'=4] {'gy_0'}, use_global_device_ids=true, to_apply=%region_9.0 | all-reduce | flops 1 | bytes 8 | tf_op jit(solution)/shard_map/psum | solution.py:32
  351.2 9.9 %psum.39 = f32[]{:T(128)} all-reduce(f32[]{:T(128)} %psum.38), channel_id=1, replica_groups=mesh['gx_0'=4,'gx_1'=2,'gx_2'=2,'gy_0'=4,'gy_1'=4] {'gy_1'}, use_global_device_ids=true, to_apply=%region_10.0 | all-reduce | flops 1 | bytes 8 | tf_op jit(solution)/shard_map/psum | solution.py:32
  361.8 1.1 fusion.20
  362.9 0.7 maximum_bitcast_fusion
  363.6 0.0 all-gather.9.cloned.1.call-update
  363.6 55.2 %all-gather.9.cloned.1.call-done = bf16[16,320,160]{1,2,0:T(8,128)(2,1)} async-done(((bf16[1,320,160]{1,2,0:T(8,128)(2,1)}), bf16[16,320,160]{1,2,0:T(8,128)(2,1)}) %all-gather.9.cloned.1.call-update) | async-done | bytes 1638416 | tf_op jit(solution)/shard_map/all_gather | solution.py:40
  418.8 2.2 copy.21
  421.1 0.0 copy-start.1
  421.1 2.5 reshape.30
  423.6 1.7 convert_bitcast_fusion
  425.4 1.8 fusion.35
  (12 shorter events, 0.0 us)
Async XLA Ops:
  7.2 6.9 %copy-start = (bf16[16,1280]{1,0:T(8,128)(2,1)S(1)}, bf16[16,1280]{1,0:T(8,128)(2,1)}, u32[]{:S(2)}) copy-start(bf16[16,1280]{1,0:T(8,128)(2,1)} %param.18) | copy-start | bytes 122884
  7.2 6.8 %copy-start.4 = (s32[512]{0:T(512)S(1)}, s32[512]{0:T(512)}, u32[]{:S(2)}) copy-start(s32[512]{0:T(512)} %param.16) | copy-start | bytes 6148
  7.2 52.1 %all-gather.5.cloned.1.call-start = ((), (), s32[]{:S(2)}) async-start(), calls=%async_computation.2 | async-start | bytes 6963200 | tf_op jit(solution)/shard_map/all_gather | solution.py:101
  9.2 99.4 %all-gather.7.cloned.1.call-start = ((), (), s32[]{:S(2)}) async-start(), calls=%async_computation.3 | async-start | bytes 6963200 | tf_op jit(solution)/shard_map/all_gather | solution.py:108
  11.2 270.8 %reduce-scatter.2.cloned.1.call-start = ((), (), s32[]{:S(2)}) async-start(), calls=%async_computation.4 | async-start | bytes 13926400 | tf_op jit(solution)/shard_map/reduce_scatter | solution.py:113
  12.1 3.1 copy-start.5
  12.1 47.2 %copy-start.7 = (f32[1280]{0:T(1024)S(1)}, f32[1280]{0:T(1024)}, u32[]{:S(2)}) copy-start(f32[1280]{0:T(1024)} %param.19) | copy-start | bytes 15364
  59.3 8.4 %copy-start.6 = (bf16[512,1280]{1,0:T(8,128)(2,1)S(1)}, bf16[512,1280]{1,0:T(8,128)(2,1)}, u32[]{:S(2)}) copy-start(bf16[512,1280]{1,0:T(8,128)(2,1)} %param.13) | copy-start | bytes 3932164
  65.3 2.4 copy-start.8
  135.2 226.5 %copy-start.2 = (f32[80,2560]{1,0:T(8,128)S(1)}, f32[80,2560]{1,0:T(8,128)}, u32[]{:S(2)}) copy-start(f32[80,2560]{1,0:T(8,128)} %param.20) | copy-start | bytes 2457604
  135.2 226.5 %copy-start.3 = (f32[80,2560]{1,0:T(8,128)S(1)}, f32[80,2560]{1,0:T(8,128)}, u32[]{:S(2)}) copy-start(f32[80,2560]{1,0:T(8,128)} %param.21) | copy-start | bytes 2457604
  285.1 32.2 %all-to-all-start = ((bf16[16,80,320]{2,1,0:T(8,128)(2,1)}), bf16[16,80,320]{2,1,0:T(8,128)(2,1)S(1)}, u32[]{:S(2)}, u32[]{:S(2)}) async-start(bf16[16,80,320]{2,1,0:T(8,128)(2,1)} %bitcast.24), calls=%async_computation.1 | async-start | bytes 1966080 | tf_op jit(solution)/shard_map/all_to_all | solution.py:26
  293.8 125.0 %all-gather.9.cloned.1.call-start = ((), (), s32[]{:S(2)}) async-start(), calls=%async_computation.5 | async-start | bytes 2088960 | tf_op jit(solution)/shard_map/all_gather | solution.py:40
  421.1 6.0 %copy-start.1 = (bf16[16,1280]{1,0:T(8,128)(2,1)S(1)}, bf16[16,1280]{1,0:T(8,128)(2,1)}, u32[]{:S(2)}) copy-start(bf16[16,1280]{1,0:T(8,128)(2,1)} %param.18) | copy-start | bytes 122884
Sparse Core Ops, SparseCore 0:
  10.4 48.8 all-gather.4
  61.7 46.8 all-gather.6
  135.3 146.6 reduce-scatter.1
  363.7 55.0 all-gather.8
where the time goes:
time: 434 us
  waiting for transfers between devices  304 us (70%)
  blocking collectives  42.9 us (10%)
  matrix products  29.1 us (7%)
  other arithmetic  21.6 us (5%)
  between operations  14.6 us (3%)
  local copies, waits for them, and re-layouts  12 us (3%)
  starting transfers between devices  9.01 us (2%)
    reduce_scatter x1, waiting for transfers between devices, on_device(): lax.psum_scatter(jnp.concatenate([column_product(normed, pre_grad), colum...  147 us
    all_gather x1, waiting for transfers between devices, gather_turned(): out = lax.all_gather(both, axis, axis=0, tiled=True)  55.2 us
    all_gather x1, waiting for transfers between devices, on_device(): lax.all_gather(master_up.astype(jnp.bfloat16), GX, axis=0, tiled=True)  44 us
    psum x5, blocking collectives, over_axes(): value = lax.psum(value, axis)  42.9 us
    all_gather x1, waiting for transfers between devices, on_device(): lax.all_gather(master_down.astype(jnp.bfloat16), GX, axis=0, tiled=True)  34.9 us
    all_to_all x1, waiting for transfers between devices, sent_and_summed(): pieces = lax.all_to_all(in_blocks(value, dim, size), axis, 0, 0, tiled=True)  23.3 us
    dot_general x2, matrix products, column_product(): lax.dot_general(left, right, (((0,), (0,)), ((), ())), preferred_element_...  20.4 us
    concatenate x1, other arithmetic, on_device(): jnp.concatenate([column_product(normed, pre_grad), column_product(weighte...  12.2 us
  transfers between devices with their start and end apart: 5, of which 5 were waited for; matrix products, arithmetic and copies ran while one was open for 4% of the time, Pallas kernels for 0%

commit v1 on v0

--- a/solution.py
+++ b/solution.py
@@ -98,7 +98,12 @@
     left_cols = normed
     pre_act = jnp.dot(
         left_cols,
-        lax.all_gather(master_up.astype(jnp.bfloat16), GX, axis=0, tiled=True),
+        jnp.concatenate(
+            lax.all_to_all(
+                jnp.stack([master_up.astype(jnp.bfloat16)] * lax.axis_size(GX)), GX, 0, 0
+            ),
+            axis=0,
+        ),
         preferred_element_type=jnp.float32,
     )
     hidden = gelu_tanh(pre_act).astype(jnp.bfloat16)

time: 434 us -> 474 us (1.092)
  waiting for transfers between devices: 304 us -> 338 us
  starting transfers between devices: 9.01 us -> 15.6 us
    all_to_all x0 -> x1, waiting for transfers between devices: none -> 101 us  [on_device(): lax.all_to_all(jnp.stack([master_up.astype(jnp.bfloat16)] * lax.axis_size...]
    all_gather x1 -> x0, waiting for transfers between devices: 44 us -> none  [on_device(): lax.all_gather(master_up.astype(jnp.bfloat16), GX, axis=0, tiled=True)]
    all_gather x1, waiting for transfers between devices: 34.9 us -> 0.01 us  [on_device(): lax.all_gather(master_down.astype(jnp.bfloat16), GX, axis=0, tiled=True)]
    reduce_scatter x1, waiting for transfers between devices: 147 us -> 158 us  [on_device(): lax.psum_scatter(jnp.concatenate([column_product(normed, pre_grad), colum...]
    all_to_all x0 -> x1, starting transfers between devices: none -> 6.8 us  [on_device(): lax.all_to_all(jnp.stack([master_up.astype(jnp.bfloat16)] * lax.axis_size...]
  transfers between devices with their start and end apart: 5 -> 5, of which waited for: 5 -> 4; matrix products, arithmetic and copies ran while one was open for 4% -> 3% of each run, Pallas kernels for 0% -> 0%
where the time goes in v1:
time: 474 us; the launch traced here: 473 us
  waiting for transfers between devices  338 us (71%)
  blocking collectives  43 us (9%)
  matrix products  27.8 us (6%)
  other arithmetic  19.1 us (4%)
  starting transfers between devices  15.6 us (3%)
  local copies, waits for them, and re-layouts  15.3 us (3%)
  between operations  14.6 us (3%)
    reduce_scatter x1, waiting for transfers between devices, on_device(): lax.psum_scatter(jnp.concatenate([column_product(normed, pre_grad), colum...  158 us
    all_to_all x1, waiting for transfers between devices, on_device(): lax.all_to_all(jnp.stack([master_up.astype(jnp.bfloat16)] * lax.axis_size...  101 us
    all_gather x1, waiting for transfers between devices, gather_turned(): out = lax.all_gather(both, axis, axis=0, tiled=True)  55.3 us
    psum x5, blocking collectives, over_axes(): value = lax.psum(value, axis)  43 us
    all_to_all x1, waiting for transfers between devices, sent_and_summed(): pieces = lax.all_to_all(in_blocks(value, dim, size), axis, 0, 0, tiled=True)  23.5 us
    dot_general x2, matrix products, column_product(): lax.dot_general(left, right, (((0,), (0,)), ((), ())), preferred_element_...  20.4 us
    concatenate x1, other arithmetic, on_device(): jnp.concatenate([column_product(normed, pre_grad), column_product(weighte...  12.2 us
  transfers between devices with their start and end apart: 5, of which 4 were waited for; matrix products, arithmetic and copies ran while one was open for 3% of the time, Pallas kernels for 0%

profile of v1, /device:TPU:2, one launch (start us, length us, event | category | flops | bytes accessed | tf_op | source)
XLA Modules:
  0.0 473.5 jit_solution(3021008525462435188)
XLA Ops:
  7.2 0.0 copy-start
  7.2 1.2 convert_element_type.53
  8.4 3.3 stack.2
  11.7 0.0 copy-start.6
  11.7 6.8 %all-to-all-start = ((bf16[16,80,2560]{2,1,0:T(8,128)(2,1)}), bf16[16,80,2560]{2,1,0:T(8,128)(2,1)}, u32[]{:S(2)}, u32[]{:S(2)}) async-start(bf16[16,80,2560]{2,1,0:T(8,128)(2,1)} %stack.2), calls=%async_computation | async-start | bytes 13107200 | tf_op jit(solution)/shard_map/all_to_all | solution.py:102
  18.5 0.0 all-gather.4.cloned.1.call-start
  18.6 0.8 convert_element_type.57
  19.4 0.0 all-gather.4.cloned.1.call-update
  19.4 0.0 reduce-scatter.2.cloned.1.call-start
  19.5 0.0 copy-done.8
  19.5 0.1 convert_reduce_fusion.1
  19.6 0.0 copy-done.4
  19.6 0.0 copy-start.10
  19.6 0.6 convolution_add_fusion.1
  20.2 0.7 fusion.37
  20.9 0.4 multiply_reduce_fusion
  21.3 0.1 fusion.21
  21.4 100.7 %all-to-all-done = bf16[16,80,2560]{2,1,0:T(8,128)(2,1)} async-done(((bf16[16,80,2560]{2,1,0:T(8,128)(2,1)}), bf16[16,80,2560]{2,1,0:T(8,128)(2,1)}, u32[]{:S(2)}, u32[]{:S(2)}) %all-to-all-start) | async-done | bytes 6553632 | tf_op jit(solution)/shard_map/all_to_all | solution.py:102
  122.1 6.1 %fusion.33 = f32[512,2560]{1,0:T(8,128)S(1)} fusion(bf16[1280,2560]{1,0:T(8,128)(2,1)} %bitcast, f32[512,1280]{1,0:T(8,128)S(1)} %get-tuple-element.13, f32[1280]{0:T(1024)S(1)} %copy-done.10, f32[512]{0:T(512)S(1)} %add_rsqrt_fusion, f32[512]{0:T(512)S(1)} %broadcast_multiply_fusion), kind=kOutput, calls=%fused_computation.63 | convolution fusion | flops 3358064640 | bytes 14427136 | tf_op jit(solution)/shard_map/dot_general | solution.py:99
  128.2 0.0 copy-start.11
  128.2 2.4 copy-done.11
  130.6 6.0 %convolution_convert_fusion = bf16[1280,2560]{1,0:T(8,128)(2,1)} fusion(f32[512,2560]{1,0:T(8,128)S(1)} %fusion.33, bf16[512,1280]{1,0:T(8,128)(2,1)S(1)} %copy-done.9, f32[512]{0:T(512)S(1)} %bitcast.29), kind=kOutput, calls=%fused_computation.1 | convolution fusion | flops 3372482560 | bytes 13109248 | tf_op jit(solution)/shard_map/dot_general | solution.py:64
  136.6 14.3 %convolution_convert_fusion.1 = bf16[1280,2560]{1,0:T(8,128)(2,1)} fusion(f32[512,2560]{1,0:T(8,128)} %copy-done.11, bf16[1280,2560]{1,0:T(8,128)(2,1)} %all-gather.4.cloned.1.call-done, bf16[512,1280]{1,0:T(8,128)(2,1)} %param.13, f32[512]{0:T(512)S(1)} %bitcast.30, f32[512,1280]{1,0:T(8,128)S(1)} %get-tuple-element.13, f32[1280]{0:T(1024)S(1)} %copy-done.10, ...), kind=kOutput, calls=%fused_computation.2 | convolution fusion | flops 6750208000 | bytes 22293504 | tf_op jit(solution)/shard_map/dot_general | solution.py:64
  151.0 12.2 %pad_maximum_fusion = bf16[1280,5120]{1,0:T(8,128)(2,1)} fusion(bf16[1280,2560]{1,0:T(8,128)(2,1)} %convolution_convert_fusion, bf16[1280,2560]{1,0:T(8,128)(2,1)} %convolution_convert_fusion.1), kind=kLoop, calls=%fused_computation | loop fusion | flops 26214400 | bytes 26214400 | tf_op jit(solution)/shard_map/concatenate | solution.py:119
  163.2 0.0 reduce-scatter.2.cloned.1.call-update
  163.2 0.0 copy-start.3
  163.2 158.5 %reduce-scatter.2.cloned.1.call-done = bf16[80,5120]{1,0:T(8,128)(2,1)} async-done(((bf16[1280,5120]{1,0:T(8,128)(2,1)}), bf16[80,5120]{1,0:T(8,128)(2,1)}) %reduce-scatter.2.cloned.1.call-update) | async-done | bytes 819216 | tf_op jit(solution)/shard_map/reduce_scatter | solution.py:118
  321.7 1.9 reshape.34
  323.6 1.2 copy.23
  324.8 8.7 %all-to-all-start.1 = ((bf16[16,80,320]{2,1,0:T(8,128)(2,1)}), bf16[16,80,320]{2,1,0:T(8,128)(2,1)S(1)}, u32[]{:S(2)}, u32[]{:S(2)}) async-start(bf16[16,80,320]{2,1,0:T(8,128)(2,1)} %bitcast.25), calls=%async_computation.2 | async-start | bytes 1966080 | tf_op jit(solution)/shard_map/all_to_all | solution.py:26
  333.4 0.0 all-gather.6.cloned.1.call-start
  333.5 23.5 %all-to-all-done.1 = bf16[16,80,320]{2,1,0:T(8,128)(2,1)S(1)} async-done(((bf16[16,80,320]{2,1,0:T(8,128)(2,1)}), bf16[16,80,320]{2,1,0:T(8,128)(2,1)S(1)}, u32[]{:S(2)}, u32[]{:S(2)}) %all-to-all-start.1) | async-done | bytes 819232 | tf_op jit(solution)/shard_map/all_to_all | solution.py:26
  357.0 0.2 convert_reduce_fusion
  357.2 0.6 multiply_reduce_fusion.1
  357.8 15.4 %psum.35 = f32[]{:T(128)} all-reduce(f32[]{:T(128)} %multiply_reduce_fusion.1), channel_id=1, replica_groups=mesh['gx_0'=4,'gx_1'=2,'gx_2'=2,'gy_0'=4,'gy_1'=4] {'gx_0'}, use_global_device_ids=true, to_apply=%region_6.0 | all-reduce | flops 1 | bytes 8 | tf_op jit(solution)/shard_map/psum | solution.py:32
  373.2 5.5 %psum.36 = f32[]{:T(128)} all-reduce(f32[]{:T(128)} %psum.35), channel_id=1, replica_groups=mesh['gx_0'=4,'gx_1'=2,'gx_2'=2,'gy_0'=4,'gy_1'=4] {'gx_1'}, use_global_device_ids=true, to_apply=%region_7.0 | all-reduce | flops 1 | bytes 8 | tf_op jit(solution)/shard_map/psum | solution.py:32
  378.8 3.1 psum.37
  381.9 9.2 %psum.38 = f32[]{:T(128)} all-reduce(f32[]{:T(128)} %psum.37), channel_id=1, replica_groups=mesh['gx_0'=4,'gx_1'=2,'gx_2'=2,'gy_0'=4,'gy_1'=4] {'gy_0'}, use_global_device_ids=true, to_apply=%region_9.0 | all-reduce | flops 1 | bytes 8 | tf_op jit(solution)/shard_map/psum | solution.py:32
  391.0 9.8 %psum.39 = f32[]{:T(128)} all-reduce(f32[]{:T(128)} %psum.38), channel_id=1, replica_groups=mesh['gx_0'=4,'gx_1'=2,'gx_2'=2,'gy_0'=4,'gy_1'=4] {'gy_1'}, use_global_device_ids=true, to_apply=%region_10.0 | all-reduce | flops 1 | bytes 8 | tf_op jit(solution)/shard_map/psum | solution.py:32
  401.5 1.1 fusion.20
  402.7 0.7 maximum_bitcast_fusion
  403.3 0.0 all-gather.6.cloned.1.call-update
  403.4 55.3 %all-gather.6.cloned.1.call-done = bf16[16,320,160]{1,2,0:T(8,128)(2,1)} async-done(((bf16[1,320,160]{1,2,0:T(8,128)(2,1)}), bf16[16,320,160]{1,2,0:T(8,128)(2,1)}) %all-gather.6.cloned.1.call-update) | async-done | bytes 1638416 | tf_op jit(solution)/shard_map/all_gather | solution.py:40
  458.7 2.2 copy.21
  460.9 0.0 copy-start.1
  460.9 2.5 reshape.36
  463.5 1.7 convert_bitcast_fusion
  465.2 1.8 fusion.35
  (18 shorter events, 0.0 us)
Async XLA Ops:
  7.2 13.0 %copy-start = (bf16[16,1280]{1,0:T(8,128)(2,1)S(1)}, bf16[16,1280]{1,0:T(8,128)(2,1)}, u32[]{:S(2)}) copy-start(bf16[16,1280]{1,0:T(8,128)(2,1)} %param.18) | copy-start | bytes 122884
  11.7 6.9 %copy-start.2 = (f32[80,2560]{1,0:T(8,128)S(1)}, f32[80,2560]{1,0:T(8,128)}, u32[]{:S(2)}) copy-start(f32[80,2560]{1,0:T(8,128)} %param.21) | copy-start | bytes 2457604
  11.7 7.8 %copy-start.8 = (s32[1,512]{1,0:T(1,128)S(1)}, s32[1,512]{1,0:T(1,128)}, u32[]{:S(2)}) copy-start(s32[1,512]{1,0:T(1,128)} %param.14) | copy-start | bytes 6148
  11.7 7.9 %copy-start.4 = (bf16[512,1280]{1,0:T(8,128)(2,1)S(1)}, bf16[512,1280]{1,0:T(8,128)(2,1)}, u32[]{:S(2)}) copy-start(bf16[512,1280]{1,0:T(8,128)(2,1)} %param.12) | copy-start | bytes 3932164
  11.7 7.9 %copy-start.5 = (bf16[16,1280]{1,0:T(8,128)(2,1)S(1)}, bf16[16,1280]{1,0:T(8,128)(2,1)}, u32[]{:S(2)}) copy-start(bf16[16,1280]{1,0:T(8,128)(2,1)} %param.17) | copy-start | bytes 122884
  11.7 7.9 %copy-start.6 = (s32[512]{0:T(512)S(1)}, s32[512]{0:T(512)}, u32[]{:S(2)}) copy-start(s32[512]{0:T(512)} %param.15) | copy-start | bytes 6148
  11.7 110.4 %all-to-all-start = ((bf16[16,80,2560]{2,1,0:T(8,128)(2,1)}), bf16[16,80,2560]{2,1,0:T(8,128)(2,1)}, u32[]{:S(2)}, u32[]{:S(2)}) async-start(bf16[16,80,2560]{2,1,0:T(8,128)(2,1)} %stack.2), calls=%async_computation | async-start | bytes 13107200 | tf_op jit(solution)/shard_map/all_to_all | solution.py:102
  18.5 1.7 copy-start.7
  18.5 118.1 %all-gather.4.cloned.1.call-start = ((), (), s32[]{:S(2)}) async-start(), calls=%async_computation.3 | async-start | bytes 6963200 | tf_op jit(solution)/shard_map/all_gather | solution.py:113
  19.4 302.3 %reduce-scatter.2.cloned.1.call-start = ((), (), s32[]{:S(2)}) async-start(), calls=%async_computation.4 | async-start | bytes 13926400 | tf_op jit(solution)/shard_map/reduce_scatter | solution.py:118
  19.6 102.5 %copy-start.10 = (f32[1280]{0:T(1024)S(1)}, f32[1280]{0:T(1024)}, u32[]{:S(2)}) copy-start(f32[1280]{0:T(1024)} %param.19) | copy-start | bytes 15364
  122.1 8.5 %copy-start.9 = (bf16[512,1280]{1,0:T(8,128)(2,1)S(1)}, bf16[512,1280]{1,0:T(8,128)(2,1)}, u32[]{:S(2)}) copy-start(bf16[512,1280]{1,0:T(8,128)(2,1)} %param.13) | copy-start | bytes 3932164
  128.2 2.4 copy-start.11
  163.2 238.3 %copy-start.3 = (f32[80,2560]{1,0:T(8,128)S(1)}, f32[80,2560]{1,0:T(8,128)}, u32[]{:S(2)}) copy-start(f32[80,2560]{1,0:T(8,128)} %param.20) | copy-start | bytes 2457604
  324.8 32.2 %all-to-all-start.1 = ((bf16[16,80,320]{2,1,0:T(8,128)(2,1)}), bf16[16,80,320]{2,1,0:T(8,128)(2,1)S(1)}, u32[]{:S(2)}, u32[]{:S(2)}) async-start(bf16[16,80,320]{2,1,0:T(8,128)(2,1)} %bitcast.25), calls=%async_computation.2 | async-start | bytes 1966080 | tf_op jit(solution)/shard_map/all_to_all | solution.py:26
  333.4 125.2 %all-gather.6.cloned.1.call-start = ((), (), s32[]{:S(2)}) async-start(), calls=%async_computation.5 | async-start | bytes 2088960 | tf_op jit(solution)/shard_map/all_gather | solution.py:40
  460.9 6.0 %copy-start.1 = (bf16[16,1280]{1,0:T(8,128)(2,1)S(1)}, bf16[16,1280]{1,0:T(8,128)(2,1)}, u32[]{:S(2)}) copy-start(bf16[16,1280]{1,0:T(8,128)(2,1)} %param.18) | copy-start | bytes 122884
Sparse Core Ops, SparseCore 0:
  21.8 109.4 all-gather.3
  163.3 158.3 reduce-scatter.1
  403.5 55.1 all-gather.5
